TPU v7x, 32 devices: a whole 2x2x4 slice. The times are simulated.
32 devices in a mesh: trial: 4 (over z), span: 4 (over y, core), heads: 2 (over x).
Axes of the slice: x: 2, y: 2, z: 4, core: 2. Of those that a mesh axis runs over, the one named last changes fastest.
Arguments:
- latents: bfloat16 [16, 1024, 512], P('trial', ('span', 'heads')), parts along dimension 0, may hold values from -6 to 6
- rotary_rows: bfloat16 [16, 1024, 64], P('trial', ('span', 'heads')), parts along dimension 0, may hold values from -6 to 6
- latent_gain: float32 [512], replicated, may hold values from 0.25 to 1.75
- key_up: bfloat16 [2048, 16, 128], P('trial', 'heads'), parts along dimension 0, may hold values from -0.25 to 0.25
- value_up: bfloat16 [2048, 16, 128], P('trial', 'heads'), parts along dimension 0, may hold values from -0.25 to 0.25
Outputs:
- cache_keys: bfloat16 [16, 16, 192, 1024], P(('trial', 'span'), 'heads'), parts along dimension 0
- cache_values: bfloat16 [16, 1024, 16, 128], P(('trial', 'span'), None, 'heads'), parts along dimension 0
There are 4 independent parts, one for each index of `trial`. A program takes and returns all parts, laid end to end along the dimension named above; an argument that names none is the same for every part. Nothing has to cross between parts.
All inputs are finite; a program needn't handle non-finite values.
Results may differ from a plain program's by a relative error of at most 0.0049.
Values may be sent and summed in bfloat16 or wider, within the bound.
A program may use at most 64 MiB of HBM per device.

v0:
```python
import jax
import jax.numpy as jnp
from jax import lax
from jax.sharding import PartitionSpec as P


def widen_rows(rows, rotary, key_up, value_up):
    wide_keys = jnp.einsum(
        "btr,rhk->bthk", rows, key_up, preferred_element_type=jnp.float32
    ).astype(jnp.bfloat16)
    shared = jnp.broadcast_to(rotary[:, :, None], wide_keys.shape[:3] + rotary.shape[2:])
    wide_values = jnp.einsum(
        "btr,rhk->bthk", rows, value_up, preferred_element_type=jnp.float32
    ).astype(jnp.bfloat16)
    return (jnp.concatenate([wide_keys, shared], axis=-1), wide_values)


def unit_rows(vectors, row_gain):
    return (
        vectors * lax.rsqrt(jnp.mean(vectors * vectors, axis=-1, keepdims=True) + 1e-06) * row_gain
    )


def shards(latents, rotary_rows, latent_gain, key_up, value_up):
    rows_ready = unit_rows(latents.astype(jnp.float32), latent_gain).astype(jnp.bfloat16)
    rows_moved, rotary_moved = (
        lax.all_to_all(rows_ready, "span", split_axis=0, concat_axis=1, tiled=True),
        lax.all_to_all(rotary_rows, "span", split_axis=0, concat_axis=1, tiled=True),
    )
    rows_cut = rows_moved.reshape(
        rows_moved.shape[0], lax.axis_size("span"), -1, rows_moved.shape[2]
    )
    rotary_cut = rotary_moved.reshape(
        rotary_moved.shape[0], lax.axis_size("span"), -1, rotary_moved.shape[2]
    )
    rows_joined, rotary_joined = (
        lax.all_gather(rows_cut, "heads", axis=2, tiled=True),
        lax.all_gather(rotary_cut, "heads", axis=2, tiled=True),
    )
    rows_whole = rows_joined.reshape(rows_joined.shape[0], -1, rows_joined.shape[3])
    rotary_whole = rotary_joined.reshape(rotary_joined.shape[0], -1, rotary_joined.shape[3])
    cache_keys, cache_values = widen_rows(rows_whole, rotary_whole, key_up, value_up)
    cache_keys = jnp.transpose(cache_keys, (0, 2, 3, 1))
    return (cache_keys, cache_values)


def solution(mesh):
    return jax.shard_map(
        shards,
        mesh=mesh,
        in_specs=(
            P("trial", ("span", "heads"), None),
            P("trial", ("span", "heads"), None),
            P(),
            P("trial", "heads", None),
            P("trial", "heads", None),
        ),
        out_specs=(
            P(("trial", "span"), "heads", None, None),
            P(("trial", "span"), None, "heads", None),
        ),
        check_vma=False,
    )
```

profile of v0, /device:TPU:0, one launch (start us, length us, event | category | flops | bytes accessed | tf_op | source)
XLA Modules:
  0.0 62.8 jit_solution(10469144401957693796)
XLA Ops:
  7.2 0.0 copy-start
  7.2 0.0 copy-start.2
  7.2 0.0 all-gather.4.cloned.1.call-start
  7.2 1.4 %fusion = f32[4,128]{1,0:T(4,128)S(1)} fusion(bf16[4,128,512]{2,1,0:T(8,128)(2,1)} %param.5), kind=kLoop, calls=%fused_computation.5 | loop fusion | flops 785920 | bytes 526336 | tf_op jit(solution)/shard_map/reduce_sum | solution.py:20
  8.6 1.2 %fusion.2 = bf16[4,128,512]{2,1,0:T(8,128)(2,1)S(1)} fusion(bf16[4,128,512]{2,1,0:T(8,128)(2,1)} %param.5, f32[512]{0:T(512)} %param.7, f32[4,128]{1,0:T(4,128)S(1)} %add_rsqrt_fusion), kind=kLoop, calls=%fused_computation.7 | loop fusion | flops 1048576 | bytes 1052672 | tf_op jit(solution)/shard_map/convert_element_type | solution.py:25
  9.8 13.0 %all_to_all.8 = bf16[4,128,512]{2,1,0:T(8,128)(2,1)} all-to-all(bf16[4,128,512]{2,1,0:T(8,128)(2,1)S(1)} %fusion.2), channel_id=1, replica_groups=mesh['trial'=4,'span'=4,'heads'=2] {'span'}, dimensions={0} | all-to-all | bytes 1048576 | tf_op jit(solution)/shard_map/all_to_all | solution.py:27
  22.8 0.0 all-gather.4.cloned.1.call-update
  22.9 3.3 %all-to-all-start.1 = ((bf16[4,128,64]{1,2,0:T(8,128)(2,1)}), bf16[4,128,64]{1,2,0:T(8,128)(2,1)S(1)}, u32[]{:S(2)}, u32[]{:S(2)}) async-start(bf16[4,128,64]{1,2,0:T(8,128)(2,1)} %param.6), calls=%async_computation.1 | async-start | bytes 131072 | tf_op jit(solution)/shard_map/all_to_all | solution.py:28
  26.2 0.0 copy-done.2
  26.2 0.7 %copy.10 = bf16[512,8,128]{0,2,1:T(8,128)(2,1)S(1)} copy(bf16[512,8,128]{2,1,0:T(8,128)(2,1)S(1)} %copy-done.2) | data formatting | bytes 2097152 | tf_op args[3]
  26.9 3.4 %all-to-all-done.1 = bf16[4,128,64]{1,2,0:T(8,128)(2,1)S(1)} async-done(((bf16[4,128,64]{1,2,0:T(8,128)(2,1)}), bf16[4,128,64]{1,2,0:T(8,128)(2,1)S(1)}, u32[]{:S(2)}, u32[]{:S(2)}) %all-to-all-start.1) | async-done | bytes 65568 | tf_op jit(solution)/shard_map/all_to_all | solution.py:28
  30.2 6.4 %all-gather.1 = bf16[4,256,64]{1,2,0:T(8,128)(2,1)S(1)} all-gather(bf16[4,128,64]{1,2,0:T(8,128)(2,1)S(1)} %all-to-all-done.1), channel_id=3, replica_groups=mesh['trial'=4,'span'=4,'heads'=2] {'heads'}, dimensions={1}, use_global_device_ids=true | all-gather | bytes 196608 | tf_op jit(solution)/shard_map/all_gather | solution.py:38
  36.6 9.6 %all-gather.4.cloned.1.call-done = bf16[4,256,512]{2,1,0:T(8,128)(2,1)} async-done(((bf16[4,128,512]{2,1,0:T(8,128)(2,1)}), bf16[4,256,512]{2,1,0:T(8,128)(2,1)}) %all-gather.4.cloned.1.call-update) | async-done | bytes 1048592 | tf_op jit(solution)/shard_map/all_gather | solution.py:37
  46.2 2.5 %fusion.4 = f32[1024,1024]{0,1:S(1)} fusion(bf16[1024,512]{1,0:T(8,128)(2,1)} %bitcast.18, bf16[512,1024]{0,1:T(8,128)(2,1)S(1)} %bitcast.17), kind=kOutput, calls=%fused_computation.10 | convolution fusion | flops 1073741824 | bytes 6291456
  48.7 0.0 copy-start.1
  48.7 0.3 convert_bitcast_fusion.1
  49.0 0.0 copy-done
  49.0 0.9 %copy-done.1 = bf16[4,256,512]{2,1,0:T(8,128)(2,1)S(1)} copy-done((bf16[4,256,512]{2,1,0:T(8,128)(2,1)S(1)}, bf16[4,256,512]{2,1,0:T(8,128)(2,1)}, u32[]{:S(2)}) %copy-start.1) | copy-done | bytes 1048600
  49.9 1.2 %convert_bitcast_fusion = bf16[1,1024,8,128]{3,1,2,0:T(8,128)(2,1)S(1)} fusion(bf16[1024,512,1]{1,0,2:T(8,128)(2,1)S(1)} %bitcast.19, bf16[512,8,128]{2,1,0:T(8,128)(2,1)S(1)} %copy-done), kind=kOutput, calls=%fused_computation.1 | convolution fusion | flops 1074790400 | bytes 4194304 | tf_op jit(solution)/shard_map/btr,rhk->bthk/dot_general | solution.py:12
  51.2 2.7 %copy.13 = bf16[1,1024,8,128]{3,2,1,0:T(8,128)(2,1)} copy(bf16[1,1024,8,128]{3,1,2,0:T(8,128)(2,1)S(1)} %convert_bitcast_fusion) | data formatting | bytes 4194304
  53.8 0.1 broadcast_in_dim.10
  54.0 2.0 %maximum_bitcast_fusion = bf16[1,8,192,1024]{3,2,1,0:T(8,128)(2,1)} fusion(bf16[1,1024,8,64]{1,3,2,0:T(8,128)(2,1)S(1)} %broadcast_in_dim.10, bf16[1,1024,8,128]{1,3,2,0:T(8,128)(2,1)S(1)} %convert_bitcast_fusion.1), kind=kLoop, calls=%fused_computation | loop fusion | flops 6291456 | bytes 6291456 | tf_op jit(solution)/shard_map/transpose | solution.py:43
  (2 shorter events, 0.0 us)
Async XLA Ops:
  7.2 41.9 %copy-start = (bf16[512,8,128]{2,1,0:T(8,128)(2,1)S(1)}, bf16[512,8,128]{2,1,0:T(8,128)(2,1)}, u32[]{:S(2)}) copy-start(bf16[512,8,128]{2,1,0:T(8,128)(2,1)} %param.9) | copy-start | bytes 3145732
  7.2 19.0 %copy-start.2 = (bf16[512,8,128]{2,1,0:T(8,128)(2,1)S(1)}, bf16[512,8,128]{2,1,0:T(8,128)(2,1)}, u32[]{:S(2)}) copy-start(bf16[512,8,128]{2,1,0:T(8,128)(2,1)} %param.8) | copy-start | bytes 3145732
  7.2 39.0 %all-gather.4.cloned.1.call-start = ((), (), s32[]{:S(2)}) async-start(), calls=%async_computation.2 | async-start | bytes 1572864 | tf_op jit(solution)/shard_map/all_gather | solution.py:37
  22.9 7.4 %all-to-all-start.1 = ((bf16[4,128,64]{1,2,0:T(8,128)(2,1)}), bf16[4,128,64]{1,2,0:T(8,128)(2,1)S(1)}, u32[]{:S(2)}, u32[]{:S(2)}) async-start(bf16[4,128,64]{1,2,0:T(8,128)(2,1)} %param.6), calls=%async_computation.1 | async-start | bytes 131072 | tf_op jit(solution)/shard_map/all_to_all | solution.py:28
  48.7 1.2 %copy-start.1 = (bf16[4,256,512]{2,1,0:T(8,128)(2,1)S(1)}, bf16[4,256,512]{2,1,0:T(8,128)(2,1)}, u32[]{:S(2)}) copy-start(bf16[4,256,512]{2,1,0:T(8,128)(2,1)} %all-gather.4.cloned.1.call-done) | copy-start | bytes 3145732
Sparse Core Ops, SparseCore 0:
  23.0 23.1 all-gather.3
where the time goes:
time: 63.1 us; the launch traced here: 62.8 us
  blocking collectives  19.3 us (31%)
  between operations  14.1 us (22%)
  waiting for transfers between devices  13 us (21%)
  other arithmetic  4.89 us (8%)
  local copies, waits for them, and re-layouts  4.37 us (7%)
  matrix products  3.75 us (6%)
  starting transfers between devices  3.33 us (5%)
    all_to_all x1, blocking collectives, shards(): lax.all_to_all(rows_ready, 'span', split_axis=0, concat_axis=1, tiled=True)  13 us
    all_gather x1, waiting for transfers between devices, shards(): lax.all_gather(rows_cut, 'heads', axis=2, tiled=True)  9.55 us
    all_gather x1, blocking collectives, shards(): lax.all_gather(rotary_cut, 'heads', axis=2, tiled=True)  6.36 us
    unnamed x8, local copies, waits for them, and re-layouts  4.24 us
    all_to_all x1, waiting for transfers between devices, shards(): lax.all_to_all(rotary_rows, 'span', split_axis=0, concat_axis=1, tiled=True)  3.39 us
    all_to_all x1, starting transfers between devices, shards(): lax.all_to_all(rotary_rows, 'span', split_axis=0, concat_axis=1, tiled=True)  3.3 us
    unnamed x1, matrix products  2.5 us
    transpose x1, other arithmetic, shards(): cache_keys = jnp.transpose(cache_keys, (0, 2, 3, 1))  1.98 us
  transfers between devices with their start and end apart: 2, of which 2 were waited for; matrix products, arithmetic and copies ran while one was open for 1% of the time, Pallas kernels for 0%

commit v1 on v0

v1 whole, which is shorter than its diff:
```python
import functools

import jax
import jax.numpy as jnp
from jax import lax
from jax.experimental import pallas as pl
from jax.experimental.pallas import tpu as pltpu
from jax.sharding import PartitionSpec as P

MESH = pl.DeviceIdType.MESH


def widen_rows(rows, rotary, key_up, value_up):
    wide_keys = jnp.einsum(
        "btr,rhk->bthk", rows, key_up, preferred_element_type=jnp.float32
    ).astype(jnp.bfloat16)
    shared = jnp.broadcast_to(rotary[:, :, None], wide_keys.shape[:3] + rotary.shape[2:])
    wide_values = jnp.einsum(
        "btr,rhk->bthk", rows, value_up, preferred_element_type=jnp.float32
    ).astype(jnp.bfloat16)
    return (jnp.concatenate([wide_keys, shared], axis=-1), wide_values)


def unit_rows(vectors, row_gain):
    return (
        vectors * lax.rsqrt(jnp.mean(vectors * vectors, axis=-1, keepdims=True) + 1e-06) * row_gain
    )


def plain_shards(latents, rotary_rows, latent_gain, key_up, value_up):
    rows_ready = unit_rows(latents.astype(jnp.float32), latent_gain).astype(jnp.bfloat16)

    def move(block):
        block = lax.all_to_all(block, "span", split_axis=0, concat_axis=1, tiled=True)
        block = block.reshape(block.shape[0], lax.axis_size("span"), -1, block.shape[2])
        block = lax.all_gather(block, "heads", axis=2, tiled=True)
        return block.reshape(block.shape[0], -1, block.shape[3])

    cache_keys, cache_values = widen_rows(move(rows_ready), move(rotary_rows), key_up, value_up)
    return (jnp.transpose(cache_keys, (0, 2, 3, 1)), cache_values)


def exchange_kernel(
    spans, lat, rot, gain, key_up, value_up, keys, values,
    stage, stage_rot, rows, turned, raw_key, raw_value, key_wide, value_wide, flat, flat_out,
    load_sem, weight_sem, send_sem, recv_sem, pass_sem, land_sem,
):
    me, side = lax.axis_index("span"), lax.axis_index("heads")
    other = 1 - side
    count, depth = lat.shape[1], lat.shape[2]
    heads, width = key_up.shape[1], key_up.shape[2]
    value_width = value_up.shape[2]
    turn = rot.shape[1]
    both = 2 * count

    def sibling(p):
        return p + 1 - 2 * lax.rem(p, 2)

    targets, sources = [sibling(me)], [sibling(me)]
    for j in range(1, spans // 2):
        ahead, behind = lax.rem(me + 2 * j, spans), lax.rem(me + spans - 2 * j, spans)
        targets += [ahead, sibling(ahead)]
        sources += [behind, lax.rem(sibling(me) + spans - 2 * j, spans)]
    steps = len(targets)

    barrier = pltpu.get_barrier_semaphore()
    for q in targets:
        pl.semaphore_signal(barrier, inc=1, device_id={"span": q}, device_id_type=MESH)
    pl.semaphore_signal(barrier, inc=1, device_id={"heads": other}, device_id_type=MESH)

    order = list(range(1, steps)) + [0]
    loads = {}
    own = (
        pltpu.make_async_copy(lat.at[me], rows.at[me, side], load_sem.at[0, steps]),
        pltpu.make_async_copy(rot.at[me], turned.at[me, side], load_sem.at[1, steps]),
    )
    for copy in own:
        copy.start()
    for i in order:
        loads[i] = (
            pltpu.make_async_copy(lat.at[targets[i]], stage.at[i], load_sem.at[0, i]),
            pltpu.make_async_copy(rot.at[targets[i]], stage_rot.at[i], load_sem.at[1, i]),
        )
        for copy in loads[i]:
            copy.start()
    weights = (
        pltpu.make_async_copy(key_up, raw_key, weight_sem.at[0]),
        pltpu.make_async_copy(value_up, raw_value, weight_sem.at[1]),
    )
    for copy in weights:
        copy.start()
    pl.semaphore_wait(barrier, steps + 1)

    def forward(q, i):
        made = []
        for k, held in enumerate((rows, turned)):
            made.append(pltpu.make_async_remote_copy(
                src_ref=held.at[q, side], dst_ref=held.at[q, side],
                send_sem=pass_sem.at[k, i], recv_sem=land_sem.at[k, i],
                device_id={"heads": other}, device_id_type=MESH,
            ))
            made[-1].start()
        return made

    for copy in own:
        copy.wait()
    passed = [forward(me, 0)]
    sent = {}
    for i in order:
        for copy in loads[i]:
            copy.wait()
        sent[i] = []
        for k, (held, land) in enumerate(((stage, rows), (stage_rot, turned))):
            sent[i].append(pltpu.make_async_remote_copy(
                src_ref=held.at[i], dst_ref=land.at[me, side],
                send_sem=send_sem.at[k, i], recv_sem=recv_sem.at[k, i],
                device_id={"span": targets[i]}, device_id_type=MESH,
            ))
            sent[i][-1].start()

    def hear(i):
        for k, (held, land) in enumerate(((stage, rows), (stage_rot, turned))):
            pltpu.make_async_remote_copy(
                src_ref=held.at[i], dst_ref=land.at[sources[i], side],
                send_sem=send_sem.at[k, i], recv_sem=recv_sem.at[k, i],
                device_id={"span": targets[i]}, device_id_type=MESH,
            ).wait_recv()
        passed.append(forward(sources[i], i + 1))

    def landed(q, i):
        for k, held in enumerate((rows, turned)):
            pltpu.make_async_remote_copy(
                src_ref=held.at[q, other], dst_ref=held.at[q, other],
                send_sem=pass_sem.at[k, i], recv_sem=land_sem.at[k, i],
                device_id={"heads": other}, device_id_type=MESH,
            ).wait_recv()

    def unravel(raw, size, put):
        piece = 128

        @pl.loop(0, depth // piece)
        def _(n):
            r = pl.multiple_of(n * piece, piece)
            part = raw[pl.ds(r, piece)].astype(jnp.float32)
            flat[pl.ds(0, piece * heads), :] = part.reshape(piece * heads, size)
            for h in range(heads):
                put(h, r, piece, flat[pl.ds(h, piece, stride=heads), :])

    def put_value(h, r, piece, block):
        value_wide[pl.ds(r, piece), h * value_width:(h + 1) * value_width] = block.astype(jnp.bfloat16)

    def put_key(h, r, piece, block):
        key_wide[h * width:(h + 1) * width, pl.ds(r, piece)] = block.T.astype(jnp.bfloat16)

    def expand(q):
        raw = rows[q].reshape(both, depth).astype(jnp.float32)
        ready = unit_rows(raw, gain[...]).astype(jnp.bfloat16)
        start = pl.multiple_of(q * both, both)
        for h in range(heads):
            wide = lax.dot_general(
                key_wide[h * width:(h + 1) * width, :], ready,
                (((1,), (1,)), ((), ())), preferred_element_type=jnp.float32,
            )
            keys[0, h, :width, pl.ds(start, both)] = wide.astype(jnp.bfloat16)
            for k in range(2):
                keys[0, h, width:width + turn, pl.ds(start + k * count, count)] = turned[q, k]
        pair = 2 * value_width
        for h in range(0, heads, 2):
            wide = jnp.dot(
                ready, value_wide[:, h * value_width:h * value_width + pair],
                preferred_element_type=jnp.float32,
            )
            for k in range(2):
                flat_out[pl.ds(h + k, both, stride=heads), :] = wide[:, k * value_width:(k + 1) * value_width]
        values[0, pl.ds(start, both)] = flat_out[...].reshape(both, heads, value_width).astype(jnp.bfloat16)

    hear(0)
    for copy in weights:
        copy.wait()
    unravel(raw_key, width, put_key)
    unravel(raw_value, value_width, put_value)
    for i in range(1, steps):
        hear(i)
        landed((me, *sources)[i - 1], i - 1)
        expand((me, *sources)[i - 1])
    for i in range(steps - 1, steps + 1):
        landed((me, *sources)[i], i)
        expand((me, *sources)[i])
    for pair in (*passed, *sent.values()):
        for copy in pair:
            copy.wait_send()


def shards(latents, rotary_rows, latent_gain, key_up, value_up):
    spans, sides = lax.axis_size("span"), lax.axis_size("heads")
    _, count, depth = latents.shape
    turn = rotary_rows.shape[2]
    heads, width, value_width = key_up.shape[1], key_up.shape[2], value_up.shape[2]
    if (
        latents.shape[0] != spans or spans % 2 or sides != 2 or count % 128 or depth % 128
        or heads % 8 or width != 128 or value_width != 128 or turn % 16
    ):
        return plain_shards(latents, rotary_rows, latent_gain, key_up, value_up)
    length = spans * sides * count
    anywhere = pl.BlockSpec(memory_space=pl.ANY)
    steps = spans - 1
    bf16 = jnp.bfloat16
    keys, values = pl.pallas_call(
        functools.partial(exchange_kernel, spans),
        out_shape=(
            jax.ShapeDtypeStruct((1, heads, width + turn, length), bf16),
            jax.ShapeDtypeStruct((1, length, heads, value_width), bf16),
        ),
        in_specs=[anywhere, anywhere, pl.BlockSpec(memory_space=pltpu.VMEM), anywhere, anywhere],
        out_specs=[pl.BlockSpec(memory_space=pltpu.VMEM)] * 2,
        scratch_shapes=[
            pltpu.VMEM((steps, count, depth), bf16),
            pltpu.VMEM((steps, turn, count), bf16),
            pltpu.VMEM((spans, sides, count, depth), bf16),
            pltpu.VMEM((spans, sides, turn, count), bf16),
            pltpu.VMEM(key_up.shape, bf16),
            pltpu.VMEM(value_up.shape, bf16),
            pltpu.VMEM((heads * width, depth), bf16),
            pltpu.VMEM((depth, heads * value_width), bf16),
            pltpu.VMEM((128 * heads, 128), jnp.float32),
            pltpu.VMEM((2 * count * heads, value_width), jnp.float32),
            pltpu.SemaphoreType.DMA((2, spans)),
            pltpu.SemaphoreType.DMA((2,)),
            pltpu.SemaphoreType.DMA((2, steps)),
            pltpu.SemaphoreType.DMA((2, steps)),
            pltpu.SemaphoreType.DMA((2, spans)),
            pltpu.SemaphoreType.DMA((2, spans)),
        ],
        compiler_params=pltpu.CompilerParams(
            collective_id=0, has_side_effects=True, vmem_limit_bytes=40 * 1024 * 1024
        ),
    )(latents, jnp.swapaxes(rotary_rows, 1, 2), latent_gain[None], key_up, value_up)
    return keys, values


def solution(mesh):
    return jax.shard_map(
        shards,
        mesh=mesh,
        in_specs=(
            P("trial", ("span", "heads"), None),
            P("trial", ("span", "heads"), None),
            P(),
            P("trial", "heads", None),
            P("trial", "heads", None),
        ),
        out_specs=(
            P(("trial", "span"), "heads", None, None),
            P(("trial", "span"), None, "heads", None),
        ),
        check_vma=False,
    )
```

time: 63.1 us -> 28.7 us (0.45)
  Pallas kernels: 0 us -> 19.7 us
  blocking collectives: 19.3 us -> 0 us
  between operations: 14.1 us -> 0.65 us
  waiting for transfers between devices: 13 us -> 0 us
  other arithmetic: 4.89 us -> 0 us
  matrix products: 3.75 us -> 0 us
  local copies, waits for them, and re-layouts: 4.37 us -> 7.99 us
  starting transfers between devices: 3.33 us -> 0 us
    pallas_call x0 -> x1, Pallas kernels: none -> 19.7 us  [shards(): pl.pallas_call(functools.partial(exchange_kernel, spans), out_shape=(jax....]
    all_to_all x1 -> x0, blocking collectives: 13 us -> none  [shards(): lax.all_to_all(rows_ready, 'span', split_axis=0, concat_axis=1, tiled=True)]
    all_gather x1 -> x0, waiting for transfers between devices: 9.55 us -> none  [shards(): lax.all_gather(rows_cut, 'heads', axis=2, tiled=True)]
    all_gather x1 -> x0, blocking collectives: 6.36 us -> none  [shards(): lax.all_gather(rotary_cut, 'heads', axis=2, tiled=True)]
    unnamed x8 -> x12, local copies, waits for them, and re-layouts: 4.24 us -> 7.99 us
    all_to_all x1 -> x0, waiting for transfers between devices: 3.39 us -> none  [shards(): lax.all_to_all(rotary_rows, 'span', split_axis=0, concat_axis=1, tiled=True)]
    all_to_all x1 -> x0, starting transfers between devices: 3.3 us -> none  [shards(): lax.all_to_all(rotary_rows, 'span', split_axis=0, concat_axis=1, tiled=True)]
    unnamed x1 -> x0, matrix products: 2.5 us -> none
  transfers between devices with their start and end apart: 2 -> 0, of which waited for: 2 -> 0; matrix products, arithmetic and copies ran while one was open for 1% -> 0% of each run, Pallas kernels for 0% -> 0%
where the time goes in v1:
time: 28.7 us; the launch traced here: 28.3 us
  Pallas kernels  19.7 us (69%)
  local copies, waits for them, and re-layouts  7.99 us (28%)
  between operations  0.65 us (2%)
    pallas_call x1, Pallas kernels, shards(): pl.pallas_call(functools.partial(exchange_kernel, spans), out_shape=(jax....  19.7 us
    unnamed x12, local copies, waits for them, and re-layouts  7.99 us

profile of v1, /device:TPU:0, one launch (start us, length us, event | category | flops | bytes accessed | tf_op | source)
XLA Modules:
  0.0 28.3 jit_solution(10906750734445642491)
XLA Ops:
  0.6 0.0 copy-start
  0.6 1.2 %copy-done = bf16[512,8,128]{2,1,0:T(8,128)(2,1)S(1)} copy-done((bf16[512,8,128]{2,1,0:T(8,128)(2,1)S(1)}, bf16[512,8,128]{2,1,0:T(8,128)(2,1)}, u32[]{:S(2)}) %copy-start) | copy-done | bytes 1048600
  1.9 0.0 copy-start.1
  1.9 1.2 %copy-done.1 = bf16[512,8,128]{2,1,0:T(8,128)(2,1)S(1)} copy-done((bf16[512,8,128]{2,1,0:T(8,128)(2,1)S(1)}, bf16[512,8,128]{2,1,0:T(8,128)(2,1)}, u32[]{:S(2)}) %copy-start.1) | copy-done | bytes 1048600
  3.1 0.0 copy-start.2
  3.1 1.0 %copy-done.2 = bf16[4,128,512]{2,1,0:T(8,128)(2,1)S(1)} copy-done((bf16[4,128,512]{2,1,0:T(8,128)(2,1)S(1)}, bf16[4,128,512]{2,1,0:T(8,128)(2,1)}, u32[]{:S(2)}) %copy-start.2) | copy-done | bytes 524312
  4.1 0.0 copy-start.3
  4.1 0.8 %copy-done.3 = bf16[4,128,64]{1,2,0:T(8,128)(2,1)S(1)} copy-done((bf16[4,128,64]{1,2,0:T(8,128)(2,1)S(1)}, bf16[4,128,64]{1,2,0:T(8,128)(2,1)}, u32[]{:S(2)}) %copy-start.3) | copy-done | bytes 65560
  5.0 0.0 copy-start.4
  5.0 0.7 %copy-done.4 = f32[512]{0:T(512)S(1)} copy-done((f32[512]{0:T(512)S(1)}, f32[512]{0:T(512)}, u32[]{:S(2)}) %copy-start.4) | copy-done | bytes 2072
  5.6 19.7 %shard_map.68 = (bf16[1,8,192,1024]{3,2,1,0:T(8,128)(2,1)S(1)}, bf16[1,1024,8,128]{3,2,1,0:T(8,128)(2,1)S(1)}) custom-call(bf16[4,128,512]{2,1,0:T(8,128)(2,1)S(1)} %copy-done.2, bf16[4,64,128]{2,1,0:T(8,128)(2,1)S(1)} %bitcast.2, f32[1,512]{1,0:T(1,128)S(1)} %bitcast.3, bf16[512,8,128]{2,1,0:T(8,128)(2,1)S(1)} %copy-done, bf16[512,8,128]{2,1,0:T(8,128)(2,1)S(1)} %copy-done.1), custom_call_target="tpu_custom_call" | custom-call | tf_op jit(solution)/shard_map/pallas_call | solution.py:208
  25.4 1.7 %copy.9 = bf16[1,8,192,1024]{3,2,1,0:T(8,128)(2,1)} copy(bf16[1,8,192,1024]{3,2,1,0:T(8,128)(2,1)S(1)} %get-tuple-element.4) | data formatting | bytes 6291456
  27.0 1.3 %copy.10 = bf16[1,1024,8,128]{3,2,1,0:T(8,128)(2,1)} copy(bf16[1,1024,8,128]{3,2,1,0:T(8,128)(2,1)S(1)} %get-tuple-element.5) | data formatting | bytes 4194304
Async XLA Ops:
  0.6 1.2 %copy-start = (bf16[512,8,128]{2,1,0:T(8,128)(2,1)S(1)}, bf16[512,8,128]{2,1,0:T(8,128)(2,1)}, u32[]{:S(2)}) copy-start(bf16[512,8,128]{2,1,0:T(8,128)(2,1)} %key_up.1) | copy-start | bytes 3145732
  1.9 1.2 %copy-start.1 = (bf16[512,8,128]{2,1,0:T(8,128)(2,1)S(1)}, bf16[512,8,128]{2,1,0:T(8,128)(2,1)}, u32[]{:S(2)}) copy-start(bf16[512,8,128]{2,1,0:T(8,128)(2,1)} %value_up.1) | copy-start | bytes 3145732
  3.1 1.0 %copy-start.2 = (bf16[4,128,512]{2,1,0:T(8,128)(2,1)S(1)}, bf16[4,128,512]{2,1,0:T(8,128)(2,1)}, u32[]{:S(2)}) copy-start(bf16[4,128,512]{2,1,0:T(8,128)(2,1)} %lat.1) | copy-start | bytes 1572868
  4.1 0.8 %copy-start.3 = (bf16[4,128,64]{1,2,0:T(8,128)(2,1)S(1)}, bf16[4,128,64]{1,2,0:T(8,128)(2,1)}, u32[]{:S(2)}) copy-start(bf16[4,128,64]{1,2,0:T(8,128)(2,1)} %param.6) | copy-start | bytes 196612
  5.0 0.7 %copy-start.4 = (f32[512]{0:T(512)S(1)}, f32[512]{0:T(512)}, u32[]{:S(2)}) copy-start(f32[512]{0:T(512)} %param.7) | copy-start | bytes 6148

commit v2 on v1

--- a/solution.py
+++ b/solution.py
@@ -41,8 +41,8 @@
 
 
 def exchange_kernel(
-    spans, lat, rot, gain, key_up, value_up, keys, values,
-    stage, stage_rot, rows, turned, raw_key, raw_value, key_wide, value_wide, flat, flat_out,
+    spans, lat, rot, far_gain, key_up, value_up, keys, values,
+    gain, stage, stage_rot, rows, turned, raw_key, raw_value, key_wide, value_wide, flat, flat_out,
     load_sem, weight_sem, send_sem, recv_sem, pass_sem, land_sem,
 ):
     me, side = lax.axis_index("span"), lax.axis_index("heads")
@@ -86,6 +86,7 @@
     weights = (
         pltpu.make_async_copy(key_up, raw_key, weight_sem.at[0]),
         pltpu.make_async_copy(value_up, raw_value, weight_sem.at[1]),
+        pltpu.make_async_copy(far_gain, gain, weight_sem.at[2]),
     )
     for copy in weights:
         copy.start()
@@ -202,7 +203,7 @@
     ):
         return plain_shards(latents, rotary_rows, latent_gain, key_up, value_up)
     length = spans * sides * count
-    anywhere = pl.BlockSpec(memory_space=pl.ANY)
+    far = pl.BlockSpec(memory_space=pltpu.HBM)
     steps = spans - 1
     bf16 = jnp.bfloat16
     keys, values = pl.pallas_call(
@@ -211,9 +212,10 @@
             jax.ShapeDtypeStruct((1, heads, width + turn, length), bf16),
             jax.ShapeDtypeStruct((1, length, heads, value_width), bf16),
         ),
-        in_specs=[anywhere, anywhere, pl.BlockSpec(memory_space=pltpu.VMEM), anywhere, anywhere],
+        in_specs=[far] * 5,
         out_specs=[pl.BlockSpec(memory_space=pltpu.VMEM)] * 2,
         scratch_shapes=[
+            pltpu.VMEM((1, depth), jnp.float32),
             pltpu.VMEM((steps, count, depth), bf16),
             pltpu.VMEM((steps, turn, count), bf16),
             pltpu.VMEM((spans, sides, count, depth), bf16),
@@ -225,7 +227,7 @@
             pltpu.VMEM((128 * heads, 128), jnp.float32),
             pltpu.VMEM((2 * count * heads, value_width), jnp.float32),
             pltpu.SemaphoreType.DMA((2, spans)),
-            pltpu.SemaphoreType.DMA((2,)),
+            pltpu.SemaphoreType.DMA((3,)),
             pltpu.SemaphoreType.DMA((2, steps)),
             pltpu.SemaphoreType.DMA((2, steps)),
             pltpu.SemaphoreType.DMA((2, spans)),

time: 28.7 us -> 28.7 us (level)
  no operation moved by 1% of the time
where the time goes in v2:
time: 28.7 us; the launch traced here: 28.4 us
  Pallas kernels  19.7 us (69%)
  local copies, waits for them, and re-layouts  7.99 us (28%)
  between operations  0.65 us (2%)
    pallas_call x1, Pallas kernels, shards(): pl.pallas_call(functools.partial(exchange_kernel, spans), out_shape=(jax....  19.7 us
    unnamed x12, local copies, waits for them, and re-layouts  7.99 us

profile of v2, /device:TPU:0, one launch (start us, length us, event | category | flops | bytes accessed | tf_op | source)
XLA Modules:
  0.0 28.4 jit_solution(1018715768882193318)
XLA Ops:
  0.6 0.0 copy-start
  0.6 1.2 %copy-done = bf16[512,8,128]{2,1,0:T(8,128)(2,1)S(1)} copy-done((bf16[512,8,128]{2,1,0:T(8,128)(2,1)S(1)}, bf16[512,8,128]{2,1,0:T(8,128)(2,1)}, u32[]{:S(2)}) %copy-start) | copy-done | bytes 1048600
  1.9 0.0 copy-start.1
  1.9 1.2 %copy-done.1 = bf16[512,8,128]{2,1,0:T(8,128)(2,1)S(1)} copy-done((bf16[512,8,128]{2,1,0:T(8,128)(2,1)S(1)}, bf16[512,8,128]{2,1,0:T(8,128)(2,1)}, u32[]{:S(2)}) %copy-start.1) | copy-done | bytes 1048600
  3.1 0.0 copy-start.2
  3.1 1.0 %copy-done.2 = bf16[4,128,512]{2,1,0:T(8,128)(2,1)S(1)} copy-done((bf16[4,128,512]{2,1,0:T(8,128)(2,1)S(1)}, bf16[4,128,512]{2,1,0:T(8,128)(2,1)}, u32[]{:S(2)}) %copy-start.2) | copy-done | bytes 524312
  4.1 0.0 copy-start.3
  4.1 0.8 %copy-done.3 = bf16[4,128,64]{1,2,0:T(8,128)(2,1)S(1)} copy-done((bf16[4,128,64]{1,2,0:T(8,128)(2,1)S(1)}, bf16[4,128,64]{1,2,0:T(8,128)(2,1)}, u32[]{:S(2)}) %copy-start.3) | copy-done | bytes 65560
  5.0 0.0 copy-start.4
  5.0 0.7 %copy-done.4 = f32[512]{0:T(512)S(1)} copy-done((f32[512]{0:T(512)S(1)}, f32[512]{0:T(512)}, u32[]{:S(2)}) %copy-start.4) | copy-done | bytes 2072
  5.6 19.7 %shard_map.68 = (bf16[1,8,192,1024]{3,2,1,0:T(8,128)(2,1)S(1)}, bf16[1,1024,8,128]{3,2,1,0:T(8,128)(2,1)S(1)}) custom-call(bf16[4,128,512]{2,1,0:T(8,128)(2,1)S(1)} %copy-done.2, bf16[4,64,128]{2,1,0:T(8,128)(2,1)S(1)} %bitcast.2, f32[1,512]{1,0:T(1,128)S(1)} %bitcast.3, bf16[512,8,128]{2,1,0:T(8,128)(2,1)S(1)} %copy-done, bf16[512,8,128]{2,1,0:T(8,128)(2,1)S(1)} %copy-done.1), custom_call_target="tpu_custom_call" | custom-call | tf_op jit(solution)/shard_map/pallas_call | solution.py:209
  25.4 1.7 %copy.9 = bf16[1,8,192,1024]{3,2,1,0:T(8,128)(2,1)} copy(bf16[1,8,192,1024]{3,2,1,0:T(8,128)(2,1)S(1)} %get-tuple-element.4) | data formatting | bytes 6291456
  27.1 1.3 %copy.10 = bf16[1,1024,8,128]{3,2,1,0:T(8,128)(2,1)} copy(bf16[1,1024,8,128]{3,2,1,0:T(8,128)(2,1)S(1)} %get-tuple-element.5) | data formatting | bytes 4194304
Async XLA Ops:
  0.6 1.2 %copy-start = (bf16[512,8,128]{2,1,0:T(8,128)(2,1)S(1)}, bf16[512,8,128]{2,1,0:T(8,128)(2,1)}, u32[]{:S(2)}) copy-start(bf16[512,8,128]{2,1,0:T(8,128)(2,1)} %key_up.1) | copy-start | bytes 3145732
  1.9 1.2 %copy-start.1 = (bf16[512,8,128]{2,1,0:T(8,128)(2,1)S(1)}, bf16[512,8,128]{2,1,0:T(8,128)(2,1)}, u32[]{:S(2)}) copy-start(bf16[512,8,128]{2,1,0:T(8,128)(2,1)} %value_up.1) | copy-start | bytes 3145732
  3.1 1.0 %copy-start.2 = (bf16[4,128,512]{2,1,0:T(8,128)(2,1)S(1)}, bf16[4,128,512]{2,1,0:T(8,128)(2,1)}, u32[]{:S(2)}) copy-start(bf16[4,128,512]{2,1,0:T(8,128)(2,1)} %lat.1) | copy-start | bytes 1572868
  4.1 0.8 %copy-start.3 = (bf16[4,128,64]{1,2,0:T(8,128)(2,1)S(1)}, bf16[4,128,64]{1,2,0:T(8,128)(2,1)}, u32[]{:S(2)}) copy-start(bf16[4,128,64]{1,2,0:T(8,128)(2,1)} %param.6) | copy-start | bytes 196612
  5.0 0.7 %copy-start.4 = (f32[512]{0:T(512)S(1)}, f32[512]{0:T(512)}, u32[]{:S(2)}) copy-start(f32[512]{0:T(512)} %param.7) | copy-start | bytes 6148

commit v3 on v2

--- a/solution.py
+++ b/solution.py
@@ -40,9 +40,43 @@
     return (jnp.transpose(cache_keys, (0, 2, 3, 1)), cache_values)
 
 
+def sibling(p):
+    return p + 1 - 2 * lax.rem(p, 2)
+
+
+def unit(raw, gain):
+    sides, count, depth = raw.shape
+    raw = raw.reshape(sides * count, depth).astype(jnp.float32)
+    return unit_rows(raw, gain[...]).astype(jnp.bfloat16)
+
+
+def expand_keys(ready, turned, key_wide, keys):
+    heads, turn, count = keys.shape[0], turned.shape[1], turned.shape[2]
+    width = keys.shape[1] - turn
+    for h in range(heads):
+        wide = lax.dot_general(
+            key_wide[h * width:(h + 1) * width, :], ready,
+            (((1,), (1,)), ((), ())), preferred_element_type=jnp.float32,
+        )
+        keys[h, :width, :] = wide.astype(jnp.bfloat16)
+        for k in range(turned.shape[0]):
+            keys[h, width:width + turn, k * count:(k + 1) * count] = turned[k]
+
+
+def expand_values(ready, value_wide, flat, values):
+    both, heads, width = values.shape
+    for h in range(0, heads, 2):
+        wide = jnp.dot(
+            ready, value_wide[:, h * width:(h + 2) * width], preferred_element_type=jnp.float32
+        )
+        for k in range(2):
+            flat[pl.ds(h + k, both, stride=heads), :] = wide[:, k * width:(k + 1) * width]
+    values[...] = flat[...].reshape(both, heads, width).astype(jnp.bfloat16)
+
+
 def exchange_kernel(
-    spans, lat, rot, far_gain, key_up, value_up, keys, values,
-    gain, stage, stage_rot, rows, turned, raw_key, raw_value, key_wide, value_wide, flat, flat_out,
+    spans, lat, rot, far_gain, key_up, value_up, keys, values, rows_last, turned_last, key_wide, value_wide, gain,
+    stage, stage_rot, rows, turned, raw_key, raw_value, flat, flat_out,
     load_sem, weight_sem, send_sem, recv_sem, pass_sem, land_sem,
 ):
     me, side = lax.axis_index("span"), lax.axis_index("heads")
@@ -52,9 +86,6 @@
     value_width = value_up.shape[2]
     turn = rot.shape[1]
     both = 2 * count
-
-    def sibling(p):
-        return p + 1 - 2 * lax.rem(p, 2)
 
     targets, sources = [sibling(me)], [sibling(me)]
     for j in range(1, spans // 2):
@@ -153,43 +184,64 @@
     def put_key(h, r, piece, block):
         key_wide[h * width:(h + 1) * width, pl.ds(r, piece)] = block.T.astype(jnp.bfloat16)
 
-    def expand(q):
-        raw = rows[q].reshape(both, depth).astype(jnp.float32)
-        ready = unit_rows(raw, gain[...]).astype(jnp.bfloat16)
-        start = pl.multiple_of(q * both, both)
-        for h in range(heads):
-            wide = lax.dot_general(
-                key_wide[h * width:(h + 1) * width, :], ready,
-                (((1,), (1,)), ((), ())), preferred_element_type=jnp.float32,
-            )
-            keys[0, h, :width, pl.ds(start, both)] = wide.astype(jnp.bfloat16)
-            for k in range(2):
-                keys[0, h, width:width + turn, pl.ds(start + k * count, count)] = turned[q, k]
-        pair = 2 * value_width
-        for h in range(0, heads, 2):
-            wide = jnp.dot(
-                ready, value_wide[:, h * value_width:h * value_width + pair],
-                preferred_element_type=jnp.float32,
-            )
-            for k in range(2):
-                flat_out[pl.ds(h + k, both, stride=heads), :] = wide[:, k * value_width:(k + 1) * value_width]
-        values[0, pl.ds(start, both)] = flat_out[...].reshape(both, heads, value_width).astype(jnp.bfloat16)
-
     hear(0)
     for copy in weights:
         copy.wait()
     unravel(raw_key, width, put_key)
     unravel(raw_value, value_width, put_value)
+    def finish(q):
+        start = pl.multiple_of(q * both, both)
+        expand_keys(
+            unit(rows[q], gain), turned.at[q], key_wide, keys.at[:, :, pl.ds(start, both)]
+        )
+        expand_values(
+            unit(rows[q], gain), value_wide, flat_out, values.at[pl.ds(start, both)]
+        )
+
     for i in range(1, steps):
         hear(i)
         landed((me, *sources)[i - 1], i - 1)
-        expand((me, *sources)[i - 1])
-    for i in range(steps - 1, steps + 1):
-        landed((me, *sources)[i], i)
-        expand((me, *sources)[i])
+        finish((me, *sources)[i - 1])
+    landed(sources[steps - 2], steps - 1)
+    finish(sources[steps - 2])
+    last = sources[steps - 1]
+    landed(last, steps)
+    rows_last[...] = rows[last]
+    turned_last[...] = turned[last]
     for pair in (*passed, *sent.values()):
         for copy in pair:
             copy.wait_send()
+
+
+def write_kernel(
+    spans, keys_part, values_part, rows_last, turned_last, key_wide, value_wide, gain,
+    keys, values, keys_last, values_last, flat, sem, last_sem,
+):
+    me = lax.axis_index("span")
+    both = values_last.shape[0]
+    order = [me, sibling(me)]
+    for j in range(1, spans // 2):
+        behind = lax.rem(me + spans - 2 * j, spans)
+        order += [behind, lax.rem(sibling(me) + spans - 2 * j, spans)]
+    copies = []
+    for i, q in enumerate(order[:-1]):
+        at = pl.ds(pl.multiple_of(q * both, both), both)
+        copies += [
+            pltpu.make_async_copy(keys_part.at[:, :, at], keys.at[0, :, :, at], sem.at[0, i]),
+            pltpu.make_async_copy(values_part.at[at], values.at[0, at], sem.at[1, i]),
+        ]
+    for copy in copies:
+        copy.start()
+    at = pl.ds(pl.multiple_of(order[-1] * both, both), both)
+    ready = unit(rows_last[...], gain)
+    expand_keys(ready, turned_last, key_wide, keys_last)
+    copies.append(pltpu.make_async_copy(keys_last, keys.at[0, :, :, at], last_sem.at[0]))
+    copies[-1].start()
+    expand_values(ready, value_wide, flat, values_last)
+    copies.append(pltpu.make_async_copy(values_last, values.at[0, at], last_sem.at[1]))
+    copies[-1].start()
+    for copy in copies:
+        copy.wait()
 
 
 def shards(latents, rotary_rows, latent_gain, key_up, value_up):
@@ -202,30 +254,34 @@
         or heads % 8 or width != 128 or value_width != 128 or turn % 16
     ):
         return plain_shards(latents, rotary_rows, latent_gain, key_up, value_up)
-    length = spans * sides * count
+    length, both = spans * sides * count, sides * count
+    steps = spans - 1
+    bf16, f32 = jnp.bfloat16, jnp.float32
+    near = pl.BlockSpec(memory_space=pltpu.VMEM)
     far = pl.BlockSpec(memory_space=pltpu.HBM)
-    steps = spans - 1
-    bf16 = jnp.bfloat16
-    keys, values = pl.pallas_call(
+    args = (latents, jnp.swapaxes(rotary_rows, 1, 2), latent_gain[None], key_up, value_up)
+    parts = pl.pallas_call(
         functools.partial(exchange_kernel, spans),
         out_shape=(
-            jax.ShapeDtypeStruct((1, heads, width + turn, length), bf16),
-            jax.ShapeDtypeStruct((1, length, heads, value_width), bf16),
+            pltpu.VMEM((heads, width + turn, length), bf16),
+            pltpu.VMEM((length, heads, value_width), bf16),
+            pltpu.VMEM((sides, count, depth), bf16),
+            pltpu.VMEM((sides, turn, count), bf16),
+            pltpu.VMEM((heads * width, depth), bf16),
+            pltpu.VMEM((depth, heads * value_width), bf16),
+            pltpu.VMEM((1, depth), f32),
         ),
         in_specs=[far] * 5,
-        out_specs=[pl.BlockSpec(memory_space=pltpu.VMEM)] * 2,
+        out_specs=[near] * 7,
         scratch_shapes=[
-            pltpu.VMEM((1, depth), jnp.float32),
             pltpu.VMEM((steps, count, depth), bf16),
             pltpu.VMEM((steps, turn, count), bf16),
             pltpu.VMEM((spans, sides, count, depth), bf16),
             pltpu.VMEM((spans, sides, turn, count), bf16),
             pltpu.VMEM(key_up.shape, bf16),
             pltpu.VMEM(value_up.shape, bf16),
-            pltpu.VMEM((heads * width, depth), bf16),
-            pltpu.VMEM((depth, heads * value_width), bf16),
-            pltpu.VMEM((128 * heads, 128), jnp.float32),
-            pltpu.VMEM((2 * count * heads, value_width), jnp.float32),
+            pltpu.VMEM((128 * heads, 128), f32),
+            pltpu.VMEM((both * heads, value_width), f32),
             pltpu.SemaphoreType.DMA((2, spans)),
             pltpu.SemaphoreType.DMA((3,)),
             pltpu.SemaphoreType.DMA((2, steps)),
@@ -236,8 +292,24 @@
         compiler_params=pltpu.CompilerParams(
             collective_id=0, has_side_effects=True, vmem_limit_bytes=40 * 1024 * 1024
         ),
-    )(latents, jnp.swapaxes(rotary_rows, 1, 2), latent_gain[None], key_up, value_up)
-    return keys, values
+    )(*(pltpu.with_memory_space_constraint(arg, pltpu.HBM) for arg in args))
+    return pl.pallas_call(
+        functools.partial(write_kernel, spans),
+        out_shape=(
+            jax.ShapeDtypeStruct((1, heads, width + turn, length), bf16),
+            jax.ShapeDtypeStruct((1, length, heads, value_width), bf16),
+        ),
+        in_specs=[near] * 7,
+        out_specs=[far] * 2,
+        scratch_shapes=[
+            pltpu.VMEM((heads, width + turn, both), bf16),
+            pltpu.VMEM((both, heads, value_width), bf16),
+            pltpu.VMEM((both * heads, value_width), f32),
+            pltpu.SemaphoreType.DMA((2, steps)),
+            pltpu.SemaphoreType.DMA((2,)),
+        ],
+        compiler_params=pltpu.CompilerParams(vmem_limit_bytes=16 * 1024 * 1024),
+    )(*parts)
 
 
 def solution(mesh):

time: 28.7 us -> 22.7 us (0.79)
  local copies, waits for them, and re-layouts: 7.99 us -> 0 us
  Pallas kernels: 19.7 us -> 21.9 us
    unnamed x12 -> x0, local copies, waits for them, and re-layouts: 7.99 us -> none
    pallas_call x1 -> x2, Pallas kernels: 19.7 us -> 21.9 us  [the longest x1 18.5 us: shards(): pl.pallas_call(functools.partial(exchange_kernel, spans), out_shape=(pltp...]
where the time goes in v3:
time: 22.7 us; the launch traced here: 22.6 us
  Pallas kernels  21.9 us (96%)
  between operations  0.64 us (3%)
    pallas_call x1, Pallas kernels, shards(): pl.pallas_call(functools.partial(exchange_kernel, spans), out_shape=(pltp...  18.5 us
    pallas_call x1, Pallas kernels, shards(): pl.pallas_call(functools.partial(write_kernel, spans), out_shape=(jax.Sha...  3.4 us

profile of v3, /device:TPU:0, one launch (start us, length us, event | category | flops | bytes accessed | tf_op | source)
XLA Modules:
  0.0 22.6 jit_solution(11397569436175990621)
XLA Ops:
  0.6 18.5 %shard_map.68 = (bf16[8,192,1024]{2,1,0:T(8,128)(2,1)S(1)}, bf16[1024,8,128]{2,1,0:T(8,128)(2,1)S(1)}, bf16[2,128,512]{2,1,0:T(8,128)(2,1)S(1)}, bf16[2,64,128]{...) custom-call(bf16[4,128,512]{2,1,0:T(8,128)(2,1)} %lat.1, ...), custom_call_target="tpu_custom_call" | custom-call | tf_op jit(solution)/shard_map/pallas_call | solution.py:263
  19.2 3.4 %shard_map.69 = (bf16[1,8,192,1024]{3,2,1,0:T(8,128)(2,1)}, bf16[1,1024,8,128]{3,2,1,0:T(8,128)(2,1)}) custom-call(bf16[8,192,1024]{2,1,0:T(8,128)(2,1)S(1)} %get-tuple-element.9.keys_part, bf16[1024,8,128]{2,1,0:T(8,128)(2,1)S(1)} %get-tuple-element.10.values_part, bf16[2,128,512]{2,1,0:T(8,128)(2,1)S(1)} %get-tuple-element.11.rows_last, ...), custom_call_target="tpu_custom_call" | custom-call | tf_op jit(solution)/shard_map/pallas_call | solution.py:296

commit v4 on v3

--- a/solution.py
+++ b/solution.py
@@ -71,7 +71,7 @@
         )
         for k in range(2):
             flat[pl.ds(h + k, both, stride=heads), :] = wide[:, k * width:(k + 1) * width]
-    values[...] = flat[...].reshape(both, heads, width).astype(jnp.bfloat16)
+    values[...] = flat[pl.ds(0, both * heads), :].reshape(both, heads, width).astype(jnp.bfloat16)
 
 
 def exchange_kernel(
@@ -202,12 +202,21 @@
         hear(i)
         landed((me, *sources)[i - 1], i - 1)
         finish((me, *sources)[i - 1])
+    last = sources[steps - 1]
+    start = pl.multiple_of(last * both + side * count, count)
+    half = pl.ds(side, 1)
+    expand_keys(
+        unit(rows[last, half], gain), turned.at[last, half], key_wide,
+        keys.at[:, :, pl.ds(start, count)],
+    )
+    expand_values(
+        unit(rows[last, half], gain), value_wide, flat_out, values.at[pl.ds(start, count)]
+    )
     landed(sources[steps - 2], steps - 1)
     finish(sources[steps - 2])
-    last = sources[steps - 1]
     landed(last, steps)
-    rows_last[...] = rows[last]
-    turned_last[...] = turned[last]
+    rows_last[...] = rows[last, pl.ds(other, 1)]
+    turned_last[...] = turned[last, pl.ds(other, 1)]
     for pair in (*passed, *sent.values()):
         for copy in pair:
             copy.wait_send()
@@ -217,22 +226,25 @@
     spans, keys_part, values_part, rows_last, turned_last, key_wide, value_wide, gain,
     keys, values, keys_last, values_last, flat, sem, last_sem,
 ):
-    me = lax.axis_index("span")
-    both = values_last.shape[0]
+    me, side = lax.axis_index("span"), lax.axis_index("heads")
+    count = values_last.shape[0]
+    both = 2 * count
     order = [me, sibling(me)]
     for j in range(1, spans // 2):
         behind = lax.rem(me + spans - 2 * j, spans)
         order += [behind, lax.rem(sibling(me) + spans - 2 * j, spans)]
+    last = order[-1] * both
+    done = [pl.ds(pl.multiple_of(q * both, both), both) for q in order[:-1]]
+    done.append(pl.ds(pl.multiple_of(last + side * count, count), count))
     copies = []
-    for i, q in enumerate(order[:-1]):
-        at = pl.ds(pl.multiple_of(q * both, both), both)
+    for i, at in enumerate(done):
         copies += [
             pltpu.make_async_copy(keys_part.at[:, :, at], keys.at[0, :, :, at], sem.at[0, i]),
             pltpu.make_async_copy(values_part.at[at], values.at[0, at], sem.at[1, i]),
         ]
     for copy in copies:
         copy.start()
-    at = pl.ds(pl.multiple_of(order[-1] * both, both), both)
+    at = pl.ds(pl.multiple_of(last + (1 - side) * count, count), count)
     ready = unit(rows_last[...], gain)
     expand_keys(ready, turned_last, key_wide, keys_last)
     copies.append(pltpu.make_async_copy(keys_last, keys.at[0, :, :, at], last_sem.at[0]))
@@ -265,8 +277,8 @@
         out_shape=(
             pltpu.VMEM((heads, width + turn, length), bf16),
             pltpu.VMEM((length, heads, value_width), bf16),
-            pltpu.VMEM((sides, count, depth), bf16),
-            pltpu.VMEM((sides, turn, count), bf16),
+            pltpu.VMEM((1, count, depth), bf16),
+            pltpu.VMEM((1, turn, count), bf16),
             pltpu.VMEM((heads * width, depth), bf16),
             pltpu.VMEM((depth, heads * value_width), bf16),
             pltpu.VMEM((1, depth), f32),
@@ -302,10 +314,10 @@
         in_specs=[near] * 7,
         out_specs=[far] * 2,
         scratch_shapes=[
-            pltpu.VMEM((heads, width + turn, both), bf16),
-            pltpu.VMEM((both, heads, value_width), bf16),
-            pltpu.VMEM((both * heads, value_width), f32),
-            pltpu.SemaphoreType.DMA((2, steps)),
+            pltpu.VMEM((heads, width + turn, count), bf16),
+            pltpu.VMEM((count, heads, value_width), bf16),
+            pltpu.VMEM((count * heads, value_width), f32),
+            pltpu.SemaphoreType.DMA((2, spans)),
             pltpu.SemaphoreType.DMA((2,)),
         ],
         compiler_params=pltpu.CompilerParams(vmem_limit_bytes=16 * 1024 * 1024),

time: 22.7 us -> 22.3 us (0.982)
  Pallas kernels: 21.9 us -> 21.5 us
    pallas_call x1, Pallas kernels: 3.4 us -> 2.94 us  [shards(): pl.pallas_call(functools.partial(write_kernel, spans), out_shape=(jax.Sha...]
where the time goes in v4:
time: 22.3 us; the launch traced here: 22.1 us
  Pallas kernels  21.5 us (96%)
  between operations  0.64 us (3%)
    pallas_call x1, Pallas kernels, shards(): pl.pallas_call(functools.partial(exchange_kernel, spans), out_shape=(pltp...  18.5 us
    pallas_call x1, Pallas kernels, shards(): pl.pallas_call(functools.partial(write_kernel, spans), out_shape=(jax.Sha...  2.94 us

profile of v4, /device:TPU:0, one launch (start us, length us, event | category | flops | bytes accessed | tf_op | source)
XLA Modules:
  0.0 22.1 jit_solution(11868789476262777128)
XLA Ops:
  0.6 18.5 %shard_map.68 = (bf16[8,192,1024]{2,1,0:T(8,128)(2,1)S(1)}, bf16[1024,8,128]{2,1,0:T(8,128)(2,1)S(1)}, bf16[1,128,512]{2,1,0:T(8,128)(2,1)S(1)}, bf16[1,64,128]{...) custom-call(bf16[4,128,512]{2,1,0:T(8,128)(2,1)} %lat.1, ...), custom_call_target="tpu_custom_call" | custom-call | tf_op jit(solution)/shard_map/pallas_call | solution.py:275
  19.2 2.9 %shard_map.69 = (bf16[1,8,192,1024]{3,2,1,0:T(8,128)(2,1)}, bf16[1,1024,8,128]{3,2,1,0:T(8,128)(2,1)}) custom-call(bf16[8,192,1024]{2,1,0:T(8,128)(2,1)S(1)} %get-tuple-element.9.keys_part, bf16[1024,8,128]{2,1,0:T(8,128)(2,1)S(1)} %get-tuple-element.10.values_part, bf16[1,128,512]{2,1,0:T(8,128)(2,1)S(1)} %get-tuple-element.11.rows_last, ...), custom_call_target="tpu_custom_call" | custom-call | tf_op jit(solution)/shard_map/pallas_call | solution.py:308

commit v5 on v4

--- a/solution.py
+++ b/solution.py
@@ -77,7 +77,7 @@
 def exchange_kernel(
     spans, lat, rot, far_gain, key_up, value_up, keys, values, rows_last, turned_last, key_wide, value_wide, gain,
     stage, stage_rot, rows, turned, raw_key, raw_value, flat, flat_out,
-    load_sem, weight_sem, send_sem, recv_sem, pass_sem, land_sem,
+    load_sem, weight_sem, send_sem, recv_sem, pass_sem, land_sem, go_sem,
 ):
     me, side = lax.axis_index("span"), lax.axis_index("heads")
     other = 1 - side
@@ -95,9 +95,12 @@
     steps = len(targets)
 
     barrier = pltpu.get_barrier_semaphore()
-    for q in targets:
-        pl.semaphore_signal(barrier, inc=1, device_id={"span": q}, device_id_type=MESH)
+    leader = spans - 1
     pl.semaphore_signal(barrier, inc=1, device_id={"heads": other}, device_id_type=MESH)
+
+    @pl.when(me != leader)
+    def _():
+        pl.semaphore_signal(barrier, inc=1, device_id={"span": leader}, device_id_type=MESH)
 
     order = list(range(1, steps)) + [0]
     loads = {}
@@ -121,7 +124,16 @@
     )
     for copy in weights:
         copy.start()
-    pl.semaphore_wait(barrier, steps + 1)
+
+    @pl.when(me == leader)
+    def _():
+        pl.semaphore_wait(barrier, spans)
+        for q in range(spans - 1):
+            pl.semaphore_signal(go_sem, inc=1, device_id={"span": q}, device_id_type=MESH)
+
+    @pl.when(me != leader)
+    def _():
+        pl.semaphore_wait(barrier, 1)
 
     def forward(q, i):
         made = []
@@ -137,6 +149,11 @@
     for copy in own:
         copy.wait()
     passed = [forward(me, 0)]
+
+    @pl.when(me != leader)
+    def _():
+        pl.semaphore_wait(go_sem, 1)
+
     sent = {}
     for i in order:
         for copy in loads[i]:
@@ -300,6 +317,7 @@
             pltpu.SemaphoreType.DMA((2, steps)),
             pltpu.SemaphoreType.DMA((2, spans)),
             pltpu.SemaphoreType.DMA((2, spans)),
+            pltpu.SemaphoreType.REGULAR,
         ],
         compiler_params=pltpu.CompilerParams(
             collective_id=0, has_side_effects=True, vmem_limit_bytes=40 * 1024 * 1024

time: 22.3 us -> 21.4 us (0.960)
  Pallas kernels: 21.5 us -> 20.6 us
    pallas_call x1, Pallas kernels: 18.5 us -> 17.6 us  [shards(): pl.pallas_call(functools.partial(exchange_kernel, spans), out_shape=(pltp...]
where the time goes in v5:
time: 21.4 us; the launch traced here: 21.2 us
  Pallas kernels  20.6 us (96%)
  between operations  0.64 us (3%)
    pallas_call x1, Pallas kernels, shards(): pl.pallas_call(functools.partial(exchange_kernel, spans), out_shape=(pltp...  17.6 us
    pallas_call x1, Pallas kernels, shards(): pl.pallas_call(functools.partial(write_kernel, spans), out_shape=(jax.Sha...  2.94 us

profile of v5, /device:TPU:0, one launch (start us, length us, event | category | flops | bytes accessed | tf_op | source)
XLA Modules:
  0.0 21.2 jit_solution(15274334762241698792)
XLA Ops:
  0.6 17.6 %shard_map.68 = (bf16[8,192,1024]{2,1,0:T(8,128)(2,1)S(1)}, bf16[1024,8,128]{2,1,0:T(8,128)(2,1)S(1)}, bf16[1,128,512]{2,1,0:T(8,128)(2,1)S(1)}, bf16[1,64,128]{...) custom-call(bf16[4,128,512]{2,1,0:T(8,128)(2,1)} %lat.1, ...), custom_call_target="tpu_custom_call" | custom-call | tf_op jit(solution)/shard_map/pallas_call | solution.py:292
  18.3 2.9 %shard_map.69 = (bf16[1,8,192,1024]{3,2,1,0:T(8,128)(2,1)}, bf16[1,1024,8,128]{3,2,1,0:T(8,128)(2,1)}) custom-call(bf16[8,192,1024]{2,1,0:T(8,128)(2,1)S(1)} %get-tuple-element.9.keys_part, bf16[1024,8,128]{2,1,0:T(8,128)(2,1)S(1)} %get-tuple-element.10.values_part, bf16[1,128,512]{2,1,0:T(8,128)(2,1)S(1)} %get-tuple-element.11.rows_last, ...), custom_call_target="tpu_custom_call" | custom-call | tf_op jit(solution)/shard_map/pallas_call | solution.py:326

commit v6 on v5

--- a/solution.py
+++ b/solution.py
@@ -139,15 +139,13 @@
         made = []
         for k, held in enumerate((rows, turned)):
             made.append(pltpu.make_async_remote_copy(
-                src_ref=held.at[q, side], dst_ref=held.at[q, side],
+                src_ref=(lat, rot)[k].at[me] if i == 0 else held.at[q, side], dst_ref=held.at[q, side],
                 send_sem=pass_sem.at[k, i], recv_sem=land_sem.at[k, i],
                 device_id={"heads": other}, device_id_type=MESH,
             ))
             made[-1].start()
         return made
 
-    for copy in own:
-        copy.wait()
     passed = [forward(me, 0)]
 
     @pl.when(me != leader)
@@ -201,6 +199,8 @@
     def put_key(h, r, piece, block):
         key_wide[h * width:(h + 1) * width, pl.ds(r, piece)] = block.T.astype(jnp.bfloat16)
 
+    for copy in own:
+        copy.wait()
     hear(0)
     for copy in weights:
         copy.wait()

time: 21.4 us -> 20.7 us (0.967)
  Pallas kernels: 20.6 us -> 19.9 us
    pallas_call x1, Pallas kernels: 17.6 us -> 17 us  [shards(): pl.pallas_call(functools.partial(exchange_kernel, spans), out_shape=(pltp...]
where the time goes in v6:
time: 20.7 us; the launch traced here: 20.6 us
  Pallas kernels  19.9 us (96%)
  between operations  0.64 us (3%)
    pallas_call x1, Pallas kernels, shards(): pl.pallas_call(functools.partial(exchange_kernel, spans), out_shape=(pltp...  17 us
    pallas_call x1, Pallas kernels, shards(): pl.pallas_call(functools.partial(write_kernel, spans), out_shape=(jax.Sha...  2.94 us

profile of v6, /device:TPU:0, one launch (start us, length us, event | category | flops | bytes accessed | tf_op | source)
XLA Modules:
  0.0 20.6 jit_solution(413090511101741122)
XLA Ops:
  0.6 17.0 %shard_map.68 = (bf16[8,192,1024]{2,1,0:T(8,128)(2,1)S(1)}, bf16[1024,8,128]{2,1,0:T(8,128)(2,1)S(1)}, bf16[1,128,512]{2,1,0:T(8,128)(2,1)S(1)}, bf16[1,64,128]{...) custom-call(bf16[4,128,512]{2,1,0:T(8,128)(2,1)} %lat.1, ...), custom_call_target="tpu_custom_call" | custom-call | tf_op jit(solution)/shard_map/pallas_call | solution.py:292
  17.6 2.9 %shard_map.69 = (bf16[1,8,192,1024]{3,2,1,0:T(8,128)(2,1)}, bf16[1,1024,8,128]{3,2,1,0:T(8,128)(2,1)}) custom-call(bf16[8,192,1024]{2,1,0:T(8,128)(2,1)S(1)} %get-tuple-element.9.keys_part, bf16[1024,8,128]{2,1,0:T(8,128)(2,1)S(1)} %get-tuple-element.10.values_part, bf16[1,128,512]{2,1,0:T(8,128)(2,1)S(1)} %get-tuple-element.11.rows_last, ...), custom_call_target="tpu_custom_call" | custom-call | tf_op jit(solution)/shard_map/pallas_call | solution.py:326

commit v7 on v6

--- a/solution.py
+++ b/solution.py
@@ -76,7 +76,7 @@
 
 def exchange_kernel(
     spans, lat, rot, far_gain, key_up, value_up, keys, values, rows_last, turned_last, key_wide, value_wide, gain,
-    stage, stage_rot, rows, turned, raw_key, raw_value, flat, flat_out,
+    rows, turned, raw_key, raw_value, flat, flat_out,
     load_sem, weight_sem, send_sem, recv_sem, pass_sem, land_sem, go_sem,
 ):
     me, side = lax.axis_index("span"), lax.axis_index("heads")
@@ -103,20 +103,12 @@
         pl.semaphore_signal(barrier, inc=1, device_id={"span": leader}, device_id_type=MESH)
 
     order = list(range(1, steps)) + [0]
-    loads = {}
     own = (
-        pltpu.make_async_copy(lat.at[me], rows.at[me, side], load_sem.at[0, steps]),
-        pltpu.make_async_copy(rot.at[me], turned.at[me, side], load_sem.at[1, steps]),
+        pltpu.make_async_copy(lat.at[me], rows.at[me, side], load_sem.at[0]),
+        pltpu.make_async_copy(rot.at[me], turned.at[me, side], load_sem.at[1]),
     )
     for copy in own:
         copy.start()
-    for i in order:
-        loads[i] = (
-            pltpu.make_async_copy(lat.at[targets[i]], stage.at[i], load_sem.at[0, i]),
-            pltpu.make_async_copy(rot.at[targets[i]], stage_rot.at[i], load_sem.at[1, i]),
-        )
-        for copy in loads[i]:
-            copy.start()
     weights = (
         pltpu.make_async_copy(key_up, raw_key, weight_sem.at[0]),
         pltpu.make_async_copy(value_up, raw_value, weight_sem.at[1]),
@@ -154,21 +146,19 @@
 
     sent = {}
     for i in order:
-        for copy in loads[i]:
-            copy.wait()
         sent[i] = []
-        for k, (held, land) in enumerate(((stage, rows), (stage_rot, turned))):
+        for k, (held, land) in enumerate(((lat, rows), (rot, turned))):
             sent[i].append(pltpu.make_async_remote_copy(
-                src_ref=held.at[i], dst_ref=land.at[me, side],
+                src_ref=held.at[targets[i]], dst_ref=land.at[me, side],
                 send_sem=send_sem.at[k, i], recv_sem=recv_sem.at[k, i],
                 device_id={"span": targets[i]}, device_id_type=MESH,
             ))
             sent[i][-1].start()
 
     def hear(i):
-        for k, (held, land) in enumerate(((stage, rows), (stage_rot, turned))):
+        for k, (held, land) in enumerate(((lat, rows), (rot, turned))):
             pltpu.make_async_remote_copy(
-                src_ref=held.at[i], dst_ref=land.at[sources[i], side],
+                src_ref=held.at[targets[i]], dst_ref=land.at[sources[i], side],
                 send_sem=send_sem.at[k, i], recv_sem=recv_sem.at[k, i],
                 device_id={"span": targets[i]}, device_id_type=MESH,
             ).wait_recv()
@@ -262,14 +252,20 @@
     for copy in copies:
         copy.start()
     at = pl.ds(pl.multiple_of(last + (1 - side) * count, count), count)
-    ready = unit(rows_last[...], gain)
-    expand_keys(ready, turned_last, key_wide, keys_last)
-    copies.append(pltpu.make_async_copy(keys_last, keys.at[0, :, :, at], last_sem.at[0]))
-    copies[-1].start()
-    expand_values(ready, value_wide, flat, values_last)
-    copies.append(pltpu.make_async_copy(values_last, values.at[0, at], last_sem.at[1]))
-    copies[-1].start()
-    for copy in copies:
+    ends = (
+        pltpu.make_async_copy(keys_last, keys.at[0, :, :, at], last_sem.at[0]),
+        pltpu.make_async_copy(values_last, values.at[0, at], last_sem.at[1]),
+    )
+
+    @pl.when(me >= 0)
+    def _():
+        ready = unit(rows_last[...], gain)
+        expand_keys(ready, turned_last, key_wide, keys_last)
+        ends[0].start()
+        expand_values(ready, value_wide, flat, values_last)
+        ends[1].start()
+
+    for copy in (*copies, *ends):
         copy.wait()
 
 
@@ -303,15 +299,13 @@
         in_specs=[far] * 5,
         out_specs=[near] * 7,
         scratch_shapes=[
-            pltpu.VMEM((steps, count, depth), bf16),
-            pltpu.VMEM((steps, turn, count), bf16),
             pltpu.VMEM((spans, sides, count, depth), bf16),
             pltpu.VMEM((spans, sides, turn, count), bf16),
             pltpu.VMEM(key_up.shape, bf16),
             pltpu.VMEM(value_up.shape, bf16),
             pltpu.VMEM((128 * heads, 128), f32),
             pltpu.VMEM((both * heads, value_width), f32),
-            pltpu.SemaphoreType.DMA((2, spans)),
+            pltpu.SemaphoreType.DMA((2,)),
             pltpu.SemaphoreType.DMA((3,)),
             pltpu.SemaphoreType.DMA((2, steps)),
             pltpu.SemaphoreType.DMA((2, steps)),

time: 20.7 us -> 20.2 us (0.976)
  Pallas kernels: 19.9 us -> 19.4 us
    pallas_call x1, Pallas kernels: 2.94 us -> 2.42 us  [shards(): pl.pallas_call(functools.partial(write_kernel, spans), out_shape=(jax.Sha...]
where the time goes in v7:
time: 20.2 us; the launch traced here: 20.1 us
  Pallas kernels  19.4 us (96%)
  between operations  0.64 us (3%)
    pallas_call x1, Pallas kernels, shards(): pl.pallas_call(functools.partial(exchange_kernel, spans), out_shape=(pltp...  17 us
    pallas_call x1, Pallas kernels, shards(): pl.pallas_call(functools.partial(write_kernel, spans), out_shape=(jax.Sha...  2.42 us

profile of v7, /device:TPU:0, one launch (start us, length us, event | category | flops | bytes accessed | tf_op | source)
XLA Modules:
  0.0 20.1 jit_solution(14725979512566169187)
XLA Ops:
  0.6 17.0 %shard_map.68 = (bf16[8,192,1024]{2,1,0:T(8,128)(2,1)S(1)}, bf16[1024,8,128]{2,1,0:T(8,128)(2,1)S(1)}, bf16[1,128,512]{2,1,0:T(8,128)(2,1)S(1)}, bf16[1,64,128]{...) custom-call(bf16[4,128,512]{2,1,0:T(8,128)(2,1)} %lat.1, ...), custom_call_target="tpu_custom_call" | custom-call | tf_op jit(solution)/shard_map/pallas_call | solution.py:288
  17.7 2.4 %shard_map.69 = (bf16[1,8,192,1024]{3,2,1,0:T(8,128)(2,1)}, bf16[1,1024,8,128]{3,2,1,0:T(8,128)(2,1)}) custom-call(bf16[8,192,1024]{2,1,0:T(8,128)(2,1)S(1)} %get-tuple-element.9.keys_part, bf16[1024,8,128]{2,1,0:T(8,128)(2,1)S(1)} %get-tuple-element.10.values_part, bf16[1,128,512]{2,1,0:T(8,128)(2,1)S(1)} %get-tuple-element.11.rows_last, ...), custom_call_target="tpu_custom_call" | custom-call | tf_op jit(solution)/shard_map/pallas_call | solution.py:320

commit v8 on v7

--- a/solution.py
+++ b/solution.py
@@ -77,7 +77,7 @@
 def exchange_kernel(
     spans, lat, rot, far_gain, key_up, value_up, keys, values, rows_last, turned_last, key_wide, value_wide, gain,
     rows, turned, raw_key, raw_value, flat, flat_out,
-    load_sem, weight_sem, send_sem, recv_sem, pass_sem, land_sem, go_sem,
+    load_sem, weight_sem, send_sem, recv_sem, pass_sem, land_sem, chip_sem, go_sem,
 ):
     me, side = lax.axis_index("span"), lax.axis_index("heads")
     other = 1 - side
@@ -98,11 +98,13 @@
     leader = spans - 1
     pl.semaphore_signal(barrier, inc=1, device_id={"heads": other}, device_id_type=MESH)
 
-    @pl.when(me != leader)
-    def _():
-        pl.semaphore_signal(barrier, inc=1, device_id={"span": leader}, device_id_type=MESH)
-
-    order = list(range(1, steps)) + [0]
+    odd = lax.rem(me, 2)
+
+    @pl.when(odd == 0)
+    def _():
+        pl.semaphore_signal(barrier, inc=1, device_id={"span": me + 1}, device_id_type=MESH)
+
+    order = list(range(steps))
     own = (
         pltpu.make_async_copy(lat.at[me], rows.at[me, side], load_sem.at[0]),
         pltpu.make_async_copy(rot.at[me], turned.at[me, side], load_sem.at[1]),
@@ -117,15 +119,22 @@
     for copy in weights:
         copy.start()
 
+    @pl.when(odd == 0)
+    def _():
+        pl.semaphore_wait(barrier, 1)
+
+    @pl.when((odd == 1) & (me != leader))
+    def _():
+        pl.semaphore_wait(barrier, 2)
+        pl.semaphore_signal(chip_sem, inc=1, device_id={"span": me - 1}, device_id_type=MESH)
+        pl.semaphore_signal(barrier, inc=1, device_id={"span": leader}, device_id_type=MESH)
+
     @pl.when(me == leader)
     def _():
-        pl.semaphore_wait(barrier, spans)
+        pl.semaphore_wait(barrier, 1 + spans // 2)
+        pl.semaphore_signal(chip_sem, inc=1, device_id={"span": leader - 1}, device_id_type=MESH)
         for q in range(spans - 1):
             pl.semaphore_signal(go_sem, inc=1, device_id={"span": q}, device_id_type=MESH)
-
-    @pl.when(me != leader)
-    def _():
-        pl.semaphore_wait(barrier, 1)
 
     def forward(q, i):
         made = []
@@ -140,12 +149,18 @@
 
     passed = [forward(me, 0)]
 
-    @pl.when(me != leader)
-    def _():
-        pl.semaphore_wait(go_sem, 1)
+    @pl.when(odd == 0)
+    def _():
+        pl.semaphore_wait(chip_sem, 1)
 
     sent = {}
     for i in order:
+        if i == 1:
+
+            @pl.when(me != leader)
+            def _():
+                pl.semaphore_wait(go_sem, 1)
+
         sent[i] = []
         for k, (held, land) in enumerate(((lat, rows), (rot, turned))):
             sent[i].append(pltpu.make_async_remote_copy(
@@ -275,7 +290,7 @@
     turn = rotary_rows.shape[2]
     heads, width, value_width = key_up.shape[1], key_up.shape[2], value_up.shape[2]
     if (
-        latents.shape[0] != spans or spans % 2 or sides != 2 or count % 128 or depth % 128
+        latents.shape[0] != spans or spans % 2 or spans < 4 or sides != 2 or count % 128 or depth % 128
         or heads % 8 or width != 128 or value_width != 128 or turn % 16
     ):
         return plain_shards(latents, rotary_rows, latent_gain, key_up, value_up)
@@ -312,6 +327,7 @@
             pltpu.SemaphoreType.DMA((2, spans)),
             pltpu.SemaphoreType.DMA((2, spans)),
             pltpu.SemaphoreType.REGULAR,
+            pltpu.SemaphoreType.REGULAR,
         ],
         compiler_params=pltpu.CompilerParams(
             collective_id=0, has_side_effects=True, vmem_limit_bytes=40 * 1024 * 1024

time: 20.2 us -> 20.8 us (1.030)
  Pallas kernels: 19.4 us -> 20 us
    pallas_call x1, Pallas kernels: 17 us -> 17.6 us  [shards(): pl.pallas_call(functools.partial(exchange_kernel, spans), out_shape=(pltp...]
where the time goes in v8:
time: 20.8 us; the launch traced here: 20.6 us
  Pallas kernels  20 us (96%)
  between operations  0.64 us (3%)
    pallas_call x1, Pallas kernels, shards(): pl.pallas_call(functools.partial(exchange_kernel, spans), out_shape=(pltp...  17.6 us
    pallas_call x1, Pallas kernels, shards(): pl.pallas_call(functools.partial(write_kernel, spans), out_shape=(jax.Sha...  2.42 us

profile of v8, /device:TPU:0, one launch (start us, length us, event | category | flops | bytes accessed | tf_op | source)
XLA Modules:
  0.0 20.6 jit_solution(5950825982728870671)
XLA Ops:
  0.6 17.6 %shard_map.68 = (bf16[8,192,1024]{2,1,0:T(8,128)(2,1)S(1)}, bf16[1024,8,128]{2,1,0:T(8,128)(2,1)S(1)}, bf16[1,128,512]{2,1,0:T(8,128)(2,1)S(1)}, bf16[1,64,128]{...) custom-call(bf16[4,128,512]{2,1,0:T(8,128)(2,1)} %lat.1, ...), custom_call_target="tpu_custom_call" | custom-call | tf_op jit(solution)/shard_map/pallas_call | solution.py:303
  18.2 2.4 %shard_map.69 = (bf16[1,8,192,1024]{3,2,1,0:T(8,128)(2,1)}, bf16[1,1024,8,128]{3,2,1,0:T(8,128)(2,1)}) custom-call(bf16[8,192,1024]{2,1,0:T(8,128)(2,1)S(1)} %get-tuple-element.9.keys_part, bf16[1024,8,128]{2,1,0:T(8,128)(2,1)S(1)} %get-tuple-element.10.values_part, bf16[1,128,512]{2,1,0:T(8,128)(2,1)S(1)} %get-tuple-element.11.rows_last, ...), custom_call_target="tpu_custom_call" | custom-call | tf_op jit(solution)/shard_map/pallas_call | solution.py:336
